TPU v7x, 32 devices: a whole 2x2x4 slice. The times are simulated.
32 devices in a mesh: batch: 8 (over y, x, core), slab: 4 (over z).
Axes of the slice: x: 2, y: 2, z: 4, core: 2. Of those that a mesh axis runs over, the one named last changes fastest.
Arguments:
- volumes: float32 [16, 128, 128, 128], P('batch', 'slab'), may hold values from -6 to 6
- tilt_low: int32 [16], P('batch'), may hold values from -70 to -40
- tilt_high: int32 [16], P('batch'), may hold values from 40 to 70
- shifts: int32 [16, 3], P('batch'), may hold values from 0 to 127
- support: float32 [128, 128, 128], P('slab'), may hold values from 0.2 to 1
Outputs:
- average: float32 [128, 128, 128], P('slab')
- misfits: float32 [3], replicated
Inputs may be any that keep to these rules, and one draw needn't show every extreme that they name: `shifts`: columns hold the shift along z, y and x.
All inputs are finite; a program needn't handle non-finite values.
Results may differ from a plain program's by a relative error of at most 0.0003.
Values sent between devices are 32-bit elements; how exact they have to be, the bound alone decides.
No kernel may reach another device: no remote copies, remote signals or barrier semaphores. Data moves between devices by JAX's collectives and lax.ppermute only.
A program may use at most 64 MiB of HBM per device.

v0:
```python
import math

import jax
import jax.numpy as jnp
from jax import lax
from jax.sharding import PartitionSpec as P

ITERS = 3


REG_WEIGHT = 0.5
FLOOR_VALUE = 1.0
SOFTNESS = 5.0
TO_DEGREES = 180.0 / math.pi
HIGHEST = lax.Precision.HIGHEST


def dft_tables(length):
    index = jnp.arange(length, dtype=jnp.int32)
    product = index[:, None] * index[None, :] % length
    angle = product.astype(jnp.float32) * (2.0 * math.pi / length)
    factor = 1.0 / math.sqrt(length)
    return (jnp.cos(angle) * factor, jnp.sin(angle) * factor)


def along(field, table, axis):
    letters = "abcd"[: field.ndim]
    target = letters[:axis] + "k" + letters[axis + 1 :]
    return jnp.einsum(
        letters + "," + letters[axis] + "k->" + target, field, table, precision=HIGHEST
    )


def forward(real_part, imag_part, tables, axis):
    cosine, sine = tables
    if imag_part is None:
        return (along(real_part, cosine, axis), -along(real_part, sine, axis))
    return (
        along(real_part, cosine, axis) + along(imag_part, sine, axis),
        along(imag_part, cosine, axis) - along(real_part, sine, axis),
    )


def backward(real_part, imag_part, tables, axis):
    cosine, sine = tables
    return (
        along(real_part, cosine, axis) - along(imag_part, sine, axis),
        along(imag_part, cosine, axis) + along(real_part, sine, axis),
    )


def signed(length):
    index = jnp.arange(length, dtype=jnp.int32)
    return jnp.where(index < length // 2, index, index - length)


def wedge(low, high, length):
    depth = signed(length)[:, None]
    across = signed(length)[None, :]
    facing = jnp.where(across >= 0, 1, -1)
    theta = (
        jnp.arctan2((depth * facing).astype(jnp.float32), jnp.abs(across).astype(jnp.float32))
        * TO_DEGREES
    )
    lower = low.astype(jnp.float32)
    upper = high.astype(jnp.float32)
    return jax.nn.sigmoid((upper - theta) / SOFTNESS) * jax.nn.sigmoid((theta - lower) / SOFTNESS)


def body(volumes, tilt_low, tilt_high, shifts, support):
    items, layer, length = (volumes.shape[0], volumes.shape[1], volumes.shape[3])
    tables = dft_tables(length)
    index = jnp.arange(length, dtype=jnp.int32)
    weights = jax.vmap(lambda low, high: wedge(low, high, length))(tilt_low, tilt_high)
    weight_square = jnp.sum(weights * weights, axis=0)
    energy = jnp.sum(volumes * volumes)
    spread = weights[:, :, None, :]
    depth_shift = shifts[:, 0][:, None, None, None]
    column_shift = shifts[:, 2][:, None, None, None]
    rolled = jax.vmap(lambda volume, offset: jnp.roll(volume, offset, axis=1))(
        volumes, shifts[:, 1]
    )
    first_real, first_imag = forward(
        lax.all_to_all(rolled, "slab", split_axis=2, concat_axis=1, tiled=True), None, tables, 3
    )
    real_part, imag_part = forward(first_real, first_imag, tables, 1)
    turns = (
        index[None, :, None, None] * depth_shift + index[None, None, None, :] * column_shift
    ) % length
    angle = turns.astype(jnp.float32) * (2.0 * math.pi / length)
    cosine = jnp.cos(angle)
    sine = jnp.sin(angle)
    part_real = jnp.sum(spread * (real_part * cosine + imag_part * sine), axis=0)
    part_imag = jnp.sum(spread * (imag_part * cosine - real_part * sine), axis=0)
    sum_real, sum_imag, weight_sum, energy_sum = lax.psum(
        (part_real, part_imag, weight_square, energy), "batch"
    )
    subs_total = items * lax.axis_size("batch")
    volume_cells = float(length * length * length)
    divisor_base = weight_sum[:, None, :]
    mean_real = jnp.zeros((length, layer, length), jnp.float32)
    mean_imag = jnp.zeros((length, layer, length), jnp.float32)
    misfits = []
    average = support
    for turn in range(ITERS):
        local = (
            energy_sum
            - 2.0 * jnp.sum(mean_real * sum_real + mean_imag * sum_imag)
            + jnp.sum(divisor_base * (mean_real * mean_real + mean_imag * mean_imag))
        )
        total = lax.psum(local, "slab")
        mean_misfit = total / (subs_total * volume_cells)
        misfits.append(mean_misfit)
        damping = REG_WEIGHT * subs_total * mean_misfit + FLOOR_VALUE
        divisor = divisor_base + damping
        new_real = mean_real + (sum_real - divisor_base * mean_real) / divisor
        new_imag = mean_imag + (sum_imag - divisor_base * mean_imag) / divisor
        real_part, imag_part = backward(new_real, new_imag, tables, 0)
        real_part, imag_part = (
            lax.all_to_all(real_part, "slab", split_axis=0, concat_axis=1, tiled=True),
            lax.all_to_all(imag_part, "slab", split_axis=0, concat_axis=1, tiled=True),
        )
        cosine_table, sine_table = tables
        average = support * (along(real_part, cosine_table, 2) - along(imag_part, sine_table, 2))
        if turn + 1 < ITERS:
            real_part, imag_part = forward(average, None, tables, 2)
            real_part, imag_part = (
                lax.all_to_all(real_part, "slab", split_axis=1, concat_axis=0, tiled=True),
                lax.all_to_all(imag_part, "slab", split_axis=1, concat_axis=0, tiled=True),
            )
            mean_real, mean_imag = forward(real_part, imag_part, tables, 0)
    return (average, jnp.stack(misfits))


def solution(mesh):
    placed = (
        P("batch", "slab", None, None),
        P("batch"),
        P("batch"),
        P("batch", None),
        P("slab", None, None),
    )
    return jax.shard_map(
        body, mesh=mesh, in_specs=placed, out_specs=(P("slab", None, None), P()), check_vma=False
    )
```

profile of v0, /device:TPU:0, one launch (start us, length us, event | category | flops | bytes accessed | tf_op | source)
XLA Modules:
  0.0 891.4 jit_solution(18313823750549226500)
XLA Ops:
  17.2 6.2 gather_fusion
  28.2 6.5 all-to-all-start
  36.5 91.6 %all-to-all-done = f32[2,32,128,128]{3,1,0,2:T(8,128)} async-done(((f32[2,32,128,128]{3,1,0,2:T(8,128)}), f32[2,32,128,128]{3,1,0,2:T(8,128)}, u32[]{:S(2)}, u32[]{:S(2)}) %all-to-all-start) | async-done | bytes 4194336 | tf_op jit(solution)/shard_map/all_to_all | solution.py:84
  151.0 9.7 %fusion.5 = (f32[128,32,128]{2,0,1:T(8,128)}, f32[128,32,128]{2,0,1:T(8,128)}) fusion(f32[128,2,32,128]{3,0,2,1:T(8,128)S(1)} %fusion.10, f32[2,128,128]{2,1,0:T(8,128)S(1)} %get-tuple-element.17, f32[2,128,128]{2,1,0:T(8,128)S(1)} %get-tuple-element.16, f32[2,128,128]{2,1,0:T(8,128)S(1)} %get-tuple-element.15, f32[128,2,32,128]{3,0,2,1:T(8,128)S(1)} %fusion.45, ...), kind=kOutput, calls=%fused_computation.9 | convolution fusion | flops 1622392832 | bytes 17170432 | tf_op jit(solution)/shard_map/abcd,bk->akcd/dot_general | solution.py:29
  164.6 14.3 %psum.51 = f32[]{:T(128)} all-reduce(f32[]{:T(128)} %multiply_reduce_fusion), channel_id=1, replica_groups=mesh['batch'=8,'slab'=4] {'batch'}, use_global_device_ids=true, to_apply=%region_5.6 | all-reduce | flops 1 | bytes 8 | tf_op jit(solution)/shard_map/psum | solution.py:95
  178.9 63.2 %all-reduce.3.cloned.1.call-done = (f32[128,32,128]{2,0,1:T(8,128)}, f32[128,128]{1,0:T(8,128)}, f32[128,32,128]{2,0,1:T(8,128)}) async-done(((f32[128,32,128]{2,0,1:T(8,128)}, f32[128,128]{1,0:T(8,128)}, f32[128,32,128]{2,0,1:T(8,128)}), (f32[128,32,128]{2,0,1:T(8,128)}, f32[128,128]{1,0:T(8,128)}, f32[128,32,128]{2,0,1:T(8,128)})) %all-reduce.3.cloned.1.call-update) | async-done | bytes 4259856 | tf_op jit(solution)/shard_map/psum | solution.py:95
  249.5 12.2 %psum.53 = f32[]{:T(128)} all-reduce(f32[]{:T(128)S(6)} %add.271), channel_id=1, replica_groups=mesh['batch'=8,'slab'=4] {'slab'}, use_global_device_ids=true, to_apply=%region_10.11 | all-reduce | flops 1 | bytes 8 | tf_op jit(solution)/shard_map/psum | solution.py:111
  282.2 37.8 %all-to-all-done.2 = f32[128,32,128]{2,1,0:T(8,128)} async-done(((f32[128,32,128]{2,1,0:T(8,128)}), f32[128,32,128]{2,1,0:T(8,128)}, u32[]{:S(2)}, u32[]{:S(2)}) %all-to-all-start.2) | async-done | bytes 2097184 | tf_op jit(solution)/shard_map/all_to_all | solution.py:121
  328.1 44.6 %all-to-all-done.1 = f32[128,32,128]{2,1,0:T(8,128)} async-done(((f32[128,32,128]{2,1,0:T(8,128)}), f32[128,32,128]{2,1,0:T(8,128)}, u32[]{:S(2)}, u32[]{:S(2)}) %all-to-all-start.1) | async-done | bytes 2097184 | tf_op jit(solution)/shard_map/all_to_all | solution.py:120
  388.0 6.1 fusion.18
  394.2 41.7 %all-to-all-done.4 = f32[32,128,128]{2,0,1:T(8,128)} async-done(((f32[32,128,128]{2,0,1:T(8,128)}), f32[32,128,128]{2,0,1:T(8,128)}, u32[]{:S(2)}, u32[]{:S(2)}) %all-to-all-start.4) | async-done | bytes 2097184 | tf_op jit(solution)/shard_map/all_to_all | solution.py:129
  443.7 44.7 %all-to-all-done.3 = f32[32,128,128]{2,0,1:T(8,128)} async-done(((f32[32,128,128]{2,0,1:T(8,128)}), f32[32,128,128]{2,0,1:T(8,128)}, u32[]{:S(2)}, u32[]{:S(2)}) %all-to-all-start.3) | async-done | bytes 2097184 | tf_op jit(solution)/shard_map/all_to_all | solution.py:128
  496.9 4.9 multiply_reduce_fusion.3
  503.7 10.6 %psum.54 = f32[]{:T(128)} all-reduce(f32[]{:T(128)S(6)} %add.279), channel_id=1, replica_groups=mesh['batch'=8,'slab'=4] {'slab'}, use_global_device_ids=true, to_apply=%region_13.14 | all-reduce | flops 1 | bytes 8 | tf_op jit(solution)/shard_map/psum | solution.py:111
  538.2 35.3 %all-to-all-done.6 = f32[128,32,128]{2,1,0:T(8,128)} async-done(((f32[128,32,128]{2,1,0:T(8,128)}), f32[128,32,128]{2,1,0:T(8,128)}, u32[]{:S(2)}, u32[]{:S(2)}) %all-to-all-start.6) | async-done | bytes 2097184 | tf_op jit(solution)/shard_map/all_to_all | solution.py:121
  573.5 4.9 all-to-all-start.5
  581.6 44.6 %all-to-all-done.5 = f32[128,32,128]{2,1,0:T(8,128)} async-done(((f32[128,32,128]{2,1,0:T(8,128)}), f32[128,32,128]{2,1,0:T(8,128)}, u32[]{:S(2)}, u32[]{:S(2)}) %all-to-all-start.5) | async-done | bytes 2097184 | tf_op jit(solution)/shard_map/all_to_all | solution.py:120
  641.5 6.1 fusion.16
  647.7 41.7 %all-to-all-done.8 = f32[32,128,128]{2,0,1:T(8,128)} async-done(((f32[32,128,128]{2,0,1:T(8,128)}), f32[32,128,128]{2,0,1:T(8,128)}, u32[]{:S(2)}, u32[]{:S(2)}) %all-to-all-start.8) | async-done | bytes 2097184 | tf_op jit(solution)/shard_map/all_to_all | solution.py:129
  697.2 44.7 %all-to-all-done.7 = f32[32,128,128]{2,0,1:T(8,128)} async-done(((f32[32,128,128]{2,0,1:T(8,128)}), f32[32,128,128]{2,0,1:T(8,128)}, u32[]{:S(2)}, u32[]{:S(2)}) %all-to-all-start.7) | async-done | bytes 2097184 | tf_op jit(solution)/shard_map/all_to_all | solution.py:128
  750.4 5.0 multiply_reduce_fusion.2
  757.4 10.3 %psum.55 = f32[]{:T(128)} all-reduce(f32[]{:T(128)S(6)} %add.289), channel_id=1, replica_groups=mesh['batch'=8,'slab'=4] {'slab'}, use_global_device_ids=true, to_apply=%region_16.17 | all-reduce | flops 1 | bytes 8 | tf_op jit(solution)/shard_map/psum | solution.py:111
  791.8 35.3 %all-to-all-done.10 = f32[128,32,128]{2,1,0:T(8,128)} async-done(((f32[128,32,128]{2,1,0:T(8,128)}), f32[128,32,128]{2,1,0:T(8,128)}, u32[]{:S(2)}, u32[]{:S(2)}) %all-to-all-start.10) | async-done | bytes 2097184 | tf_op jit(solution)/shard_map/all_to_all | solution.py:121
  836.4 42.0 %all-to-all-done.9 = f32[128,32,128]{2,1,0:T(8,128)S(1)} async-done(((f32[128,32,128]{2,1,0:T(8,128)}), f32[128,32,128]{2,1,0:T(8,128)S(1)}, u32[]{:S(2)}, u32[]{:S(2)}) %all-to-all-start.9) | async-done | bytes 2097184 | tf_op jit(solution)/shard_map/all_to_all | solution.py:120
  (131 shorter events, 202.7 us)
Async XLA Ops:
  28.2 6.7 copy-start.23
  28.2 6.7 copy-start.24
  28.2 99.9 %all-to-all-start = ((f32[2,32,128,128]{3,1,0,2:T(8,128)}), f32[2,32,128,128]{3,1,0,2:T(8,128)}, u32[]{:S(2)}, u32[]{:S(2)}) async-start(f32[2,32,128,128]{3,1,0,2:T(8,128)} %copy.46), calls=%async_computation | async-start | bytes 8388608 | tf_op jit(solution)/shard_map/all_to_all | solution.py:84
  34.6 207.4 %all-reduce.3.cloned.1.call-start = ((), (), s32[]{:S(2)}) async-start(), calls=%async_computation.11 | async-start | bytes 8519680 | tf_op jit(solution)/shard_map/psum | solution.py:95
  244.1 18.3 %copy-start.20 = (f32[128,128]{1,0:T(8,128)S(1)}, f32[128,128]{1,0:T(8,128)}, u32[]{:S(2)}) copy-start(f32[128,128]{1,0:T(8,128)} %get-tuple-element.12) | copy-start | bytes 196612
  244.1 18.3 %copy-start = (f32[128,32,128]{2,0,1:T(8,128)S(1)}, f32[128,32,128]{2,0,1:T(8,128)}, u32[]{:S(2)}) copy-start(f32[128,32,128]{2,0,1:T(8,128)} %get-tuple-element.13) | copy-start | bytes 6291460
  269.3 50.7 %all-to-all-start.2 = ((f32[128,32,128]{2,1,0:T(8,128)}), f32[128,32,128]{2,1,0:T(8,128)}, u32[]{:S(2)}, u32[]{:S(2)}) async-start(f32[128,32,128]{2,1,0:T(8,128)} %copy.58), calls=%async_computation.2 | async-start | bytes 4194304 | tf_op jit(solution)/shard_map/all_to_all | solution.py:121
  320.0 52.7 %all-to-all-start.1 = ((f32[128,32,128]{2,1,0:T(8,128)}), f32[128,32,128]{2,1,0:T(8,128)}, u32[]{:S(2)}, u32[]{:S(2)}) async-start(f32[128,32,128]{2,1,0:T(8,128)} %copy.54), calls=%async_computation.1 | async-start | bytes 4194304 | tf_op jit(solution)/shard_map/all_to_all | solution.py:120
  383.6 52.3 %all-to-all-start.4 = ((f32[32,128,128]{2,0,1:T(8,128)}), f32[32,128,128]{2,0,1:T(8,128)}, u32[]{:S(2)}, u32[]{:S(2)}) async-start(f32[32,128,128]{2,0,1:T(8,128)} %copy.63), calls=%async_computation.4 | async-start | bytes 4194304 | tf_op jit(solution)/shard_map/all_to_all | solution.py:129
  435.9 52.5 %all-to-all-start.3 = ((f32[32,128,128]{2,0,1:T(8,128)}), f32[32,128,128]{2,0,1:T(8,128)}, u32[]{:S(2)}, u32[]{:S(2)}) async-start(f32[32,128,128]{2,0,1:T(8,128)} %fusion.18), calls=%async_computation.3 | async-start | bytes 4194304 | tf_op jit(solution)/shard_map/all_to_all | solution.py:128
  496.9 4.9 copy-start.15
  515.0 4.1 copy-start.3
  515.0 4.1 copy-start.16
  524.1 49.4 %all-to-all-start.6 = ((f32[128,32,128]{2,1,0:T(8,128)}), f32[128,32,128]{2,1,0:T(8,128)}, u32[]{:S(2)}, u32[]{:S(2)}) async-start(f32[128,32,128]{2,1,0:T(8,128)} %copy.74), calls=%async_computation.6 | async-start | bytes 4194304 | tf_op jit(solution)/shard_map/all_to_all | solution.py:121
  528.5 4.7 copy-start.22
  573.5 52.7 %all-to-all-start.5 = ((f32[128,32,128]{2,1,0:T(8,128)}), f32[128,32,128]{2,1,0:T(8,128)}, u32[]{:S(2)}, u32[]{:S(2)}) async-start(f32[128,32,128]{2,1,0:T(8,128)} %copy.70), calls=%async_computation.5 | async-start | bytes 4194304 | tf_op jit(solution)/shard_map/all_to_all | solution.py:120
  637.1 52.3 %all-to-all-start.8 = ((f32[32,128,128]{2,0,1:T(8,128)}), f32[32,128,128]{2,0,1:T(8,128)}, u32[]{:S(2)}, u32[]{:S(2)}) async-start(f32[32,128,128]{2,0,1:T(8,128)} %copy.79), calls=%async_computation.8 | async-start | bytes 4194304 | tf_op jit(solution)/shard_map/all_to_all | solution.py:129
  689.4 52.5 %all-to-all-start.7 = ((f32[32,128,128]{2,0,1:T(8,128)}), f32[32,128,128]{2,0,1:T(8,128)}, u32[]{:S(2)}, u32[]{:S(2)}) async-start(f32[32,128,128]{2,0,1:T(8,128)} %fusion.16), calls=%async_computation.7 | async-start | bytes 4194304 | tf_op jit(solution)/shard_map/all_to_all | solution.py:128
  750.4 5.0 copy-start.13
  768.4 4.1 copy-start.5
  768.4 4.1 copy-start.14
  777.5 49.6 %all-to-all-start.10 = ((f32[128,32,128]{2,1,0:T(8,128)}), f32[128,32,128]{2,1,0:T(8,128)}, u32[]{:S(2)}, u32[]{:S(2)}) async-start(f32[128,32,128]{2,1,0:T(8,128)} %copy.90), calls=%async_computation.10 | async-start | bytes 4194304 | tf_op jit(solution)/shard_map/all_to_all | solution.py:121
  782.1 4.7 copy-start.21
  827.1 51.3 %all-to-all-start.9 = ((f32[128,32,128]{2,1,0:T(8,128)}), f32[128,32,128]{2,1,0:T(8,128)S(1)}, u32[]{:S(2)}, u32[]{:S(2)}) async-start(f32[128,32,128]{2,1,0:T(8,128)} %copy.86), calls=%async_computation.9 | async-start | bytes 4194304 | tf_op jit(solution)/shard_map/all_to_all | solution.py:120
  (13 other events, 28.6 us)
Sparse Core Ops, SparseCore 0:
  160.9 81.1 all-reduce.2
where the time goes:
time: 897 us; the launch traced here: 891 us
  waiting for transfers between devices  567 us (63%)
  matrix products  121 us (13%)
  local copies, waits for them, and re-layouts  62.4 us (7%)
  starting transfers between devices  51.8 us (6%)
  blocking collectives  47.4 us (5%)
  between operations  24.8 us (3%)
  other arithmetic  17 us (2%)
    all_to_all x3, waiting for transfers between devices, body(): lax.all_to_all(real_part, 'slab', split_axis=0, concat_axis=1, tiled=True)  131 us
    dot_general x36, matrix products, along(): jnp.einsum(letters + ',' + letters[axis] + 'k->' + target, field, table,...  121 us
    all_to_all x3, waiting for transfers between devices, body(): lax.all_to_all(imag_part, 'slab', split_axis=0, concat_axis=1, tiled=True)  108 us
    all_to_all x1, waiting for transfers between devices, body(): lax.all_to_all(rolled, 'slab', split_axis=2, concat_axis=1, tiled=True)  91.6 us
    all_to_all x2, waiting for transfers between devices, body(): lax.all_to_all(real_part, 'slab', split_axis=1, concat_axis=0, tiled=True)  89.3 us
    all_to_all x2, waiting for transfers between devices, body(): lax.all_to_all(imag_part, 'slab', split_axis=1, concat_axis=0, tiled=True)  83.4 us
    psum x1, waiting for transfers between devices, body(): lax.psum((part_real, part_imag, weight_square, energy), 'batch')  63.2 us
    psum x3, blocking collectives, body(): total = lax.psum(local, 'slab')  33.1 us
  transfers between devices with their start and end apart: 12, of which 12 were waited for; matrix products, arithmetic and copies ran while one was open for 7% of the time, Pallas kernels for 0%

commit v1 on v0

v1 whole, which is shorter than its diff:
```python
import functools
import math

import jax
import jax.numpy as jnp
import numpy as np
from jax import lax
from jax.experimental import pallas as pl
from jax.experimental.pallas import tpu as pltpu
from jax.sharding import PartitionSpec as P

ITERS = 3

REG_WEIGHT = 0.5
FLOOR_VALUE = 1.0
SOFTNESS = 5.0
HIGHEST = lax.Precision.HIGHEST
BF16 = jnp.bfloat16
F32 = jnp.float32
STREAMS = 2


def np_packed(n):
    half = n // 2
    row = np.arange(n)[:, None]
    lane = np.arange(n)[None, :]
    edge = (lane % half == 0) | (row < 0)
    kx = np.where(edge, lane, lane % half) + 0 * row
    kz = np.where(edge & (row > half), row - half, row + 0 * lane)
    return kz, kx, edge


def np_theta(kz, kx, n):
    signed = lambda k: np.where(k < n // 2, k, k - n)
    across = signed(kx)
    facing = np.where(across >= 0, 1, -1)
    return np.degrees(np.arctan2((signed(kz) * facing).astype(np.float64), np.abs(across))).astype(np.float32)


def np_split(table):
    high = table.astype(BF16)
    low = (table - high.astype(np.float64)).astype(BF16)
    return high, low


def np_x_forward(n):
    half = n // 2
    x = np.arange(n)[:, None]
    lane = np.arange(n)[None, :]
    angle = 2 * np.pi * ((x * (lane % half)) % n) / n
    bulk = lane % half != 0
    real, imag = np.cos(angle) * bulk, -np.sin(angle) * bulk
    left = lane < half
    plain = np.where(left, real, imag)
    turned = np.where(left, imag, -real)
    ends = np.where(lane == 0, 1.0, np.where(lane == half, (-1.0) ** x, 0.0))
    return np.concatenate([plain, turned, ends], axis=1) / math.sqrt(n)


def np_z_forward(n):
    half = n // 2
    k = np.arange(n)[:, None]
    z = np.arange(n)[None, :]
    angle = lambda k: 2 * np.pi * ((k * z) % n) / n
    packed = np.where(k <= half, np.cos(angle(k)), -np.sin(angle(k - half)))
    return np.concatenate([np.cos(angle(k)), np.sin(angle(k)), packed], axis=1) / math.sqrt(n)


def np_x_backward(n):
    half = n // 2
    lane = np.arange(n)[:, None]
    x = np.arange(n)[None, :]
    angle = 2 * np.pi * ((x * (lane % half)) % n) / n
    bulk = 2.0 * (lane % half != 0)
    left = lane < half
    first = np.where(left, np.cos(angle), -np.sin(angle)) * bulk
    second = np.where(left, np.sin(angle), np.cos(angle)) * bulk
    ends = np.where(lane == 0, 1.0, np.where(lane == half, (-1.0) ** x, 0.0))
    return np.concatenate([first, second, ends], axis=1) / math.sqrt(n)


def np_z_backward(n):
    half = n // 2
    z = np.arange(n)[:, None]
    k = np.arange(n)[None, :]
    angle = lambda k: 2 * np.pi * ((k * z) % n) / n
    count = np.where(k % half == 0, 1.0, 2.0)
    packed = count * np.where(k <= half, np.cos(angle(k)), -np.sin(angle(k - half)))
    return np.concatenate([np.cos(angle(k)), -np.sin(angle(k)), packed], axis=1) / math.sqrt(n)


def np_left(table):
    high, low = np_split(table)
    return np.concatenate([high, high, low], axis=1)


def np_right(table):
    high, low = np_split(table)
    return np.concatenate([high, high, low], axis=0)


def split_graph(table):
    high = lax.reduce_precision(table, 8, 7)
    return high.astype(BF16), (table - high).astype(BF16)


def shifted_tables(offset_z, offset_x, start, layer, n):
    half = n // 2
    step = F32(2.0 * math.pi / n)
    scale = F32(1.0 / math.sqrt(n))
    x = jnp.arange(n, dtype=jnp.int32)[None, :, None] + offset_x[:, None, None]
    wide = np.arange(3 * n)
    lane = wide % n
    part = wide // n
    kx = np.where(part < 2, lane % half, lane)
    quarter = np.select([(part == 0) & (lane < half), (part == 0), (part == 1) & (lane < half), part == 1], [0, 1, 1, 2], 0)
    keep = np.where(part < 2, lane % half != 0, lane % half == 0)
    turns = (x * jnp.asarray(kx, jnp.int32) + jnp.asarray(quarter * (n // 4), jnp.int32)) % n
    right = jnp.cos(turns.astype(F32) * step) * jnp.asarray(np.where(keep, 1.0 / math.sqrt(n), 0.0), F32)
    z = jnp.arange(layer, dtype=jnp.int32)[None, None, :] + start + offset_z[:, None, None]
    k = np.arange(n)[:, None]
    rows = [(k, 0), (k, -1), (np.where(k <= half, k, k - half), np.where(k <= half, 0, 1))]
    left = []
    for row, turn in rows:
        turns = (z * jnp.asarray(row, jnp.int32) + jnp.asarray(turn * (n // 4) + 0 * row, jnp.int32)) % n
        left.append(jnp.cos(turns.astype(F32) * step) * scale)
    right_high, right_low = split_graph(right)
    left_high, left_low = split_graph(jnp.concatenate(left, axis=2))
    return (
        jnp.concatenate([right_high, right_high, right_low], axis=1),
        jnp.concatenate([left_high, left_high, left_low], axis=2),
    )


def wedge(low, high, theta):
    lower = low.astype(F32)[:, None, None]
    upper = high.astype(F32)[:, None, None]
    return jax.nn.sigmoid((upper - theta) / SOFTNESS) * jax.nn.sigmoid((theta - lower) / SOFTNESS)


def split_value(value):
    high = value.astype(BF16)
    return high, (value - high.astype(F32)).astype(BF16)


def times_right(value, table):
    high, low = split_value(value)
    n = high.shape[1]
    return jnp.dot(jnp.concatenate([high, low], axis=1), table[: 2 * n], preferred_element_type=F32) + jnp.dot(
        high, table[2 * n :], preferred_element_type=F32
    )


def times_left(table, high, low):
    depth = high.shape[0]
    return jnp.dot(table[:, : 2 * depth], jnp.concatenate([high, low], axis=0), preferred_element_type=F32) + jnp.dot(
        table[:, 2 * depth :], high, preferred_element_type=F32
    )


def stacked(wide, n):
    return jnp.concatenate([wide[:, :n], wide[:, n : 2 * n], wide[:, 2 * n :]], axis=0)


GROUP = 8


def gather_kernel(groups_of, source_ref, right_ref, left_ref, weight_ref, *rest):
    parts = len(groups_of)
    volume_count = source_ref.shape[0]
    holders = rest[: len(rest) - parts - 2]
    outs = rest[len(holders) : len(holders) + parts]
    held, sems = rest[-2:]
    per = holders[0].shape[0]
    layer, n = held.shape[2], held.shape[3]
    planes = sum(groups_of) * GROUP

    def copy(volume, plane):
        return pltpu.make_async_copy(
            holders[volume // per].at[volume % per, :, source_ref[volume, plane], :], held.at[volume, plane], sems.at[volume, plane]
        )

    for plane in range(planes):
        for volume in range(volume_count):
            copy(volume, plane).start()

    base = 0
    for out, groups in zip(outs, groups_of):

        def one(group, carry, out=out, base=base):
            for volume in range(volume_count):
                for inner in range(GROUP):
                    copy(volume, base + group * GROUP + inner).wait()
            for volume in range(volume_count):
                rows = held[volume, pl.ds(base + group * GROUP, GROUP)].reshape(GROUP * layer, n)
                wide = times_right(rows, right_ref[volume])
                high, low = split_value(wide)
                for pair in range(GROUP // 2):
                    both = [slice((2 * pair + i) * layer, (2 * pair + i + 1) * layer) for i in range(2)]
                    spectrum = times_left(
                        left_ref[volume],
                        jnp.concatenate([stacked(high[rows_of], n) for rows_of in both], axis=1),
                        jnp.concatenate([stacked(low[rows_of], n) for rows_of in both], axis=1),
                    )
                    for i in range(2):
                        value = weight_ref[volume] * spectrum[:, i * n : (i + 1) * n]
                        at = group * GROUP + 2 * pair + i
                        out[at] = value if volume == 0 else out[at] + value
            return carry

        lax.fori_loop(0, groups, one, 0)
        base += groups * GROUP


def gather_planes(volumes, sources, right, left, weight, counts):
    volume_count, planes = sources.shape
    per, layer, n, _ = volumes[0].shape
    return pl.pallas_call(
        functools.partial(gather_kernel, tuple(count // GROUP for count in counts)),
        out_shape=[jax.ShapeDtypeStruct((count, n, n), F32) for count in counts],
        in_specs=[pl.BlockSpec(memory_space=pltpu.SMEM)]
        + [pl.BlockSpec(memory_space=pltpu.VMEM)] * 3
        + [pl.BlockSpec(memory_space=pl.ANY)] * len(volumes),
        out_specs=[pl.BlockSpec(memory_space=pltpu.VMEM)] * len(counts),
        scratch_shapes=[
            pltpu.VMEM((volume_count, planes, layer, n), F32),
            pltpu.SemaphoreType.DMA((volume_count, planes)),
        ],
        name="gather_planes",
    )(sources, right, left, weight, *volumes)


def refine_kernel(first, last, weights_of, peers, *refs):
    refs = list(refs)
    take = lambda count: [refs.pop(0) for _ in range(count)]
    (parts_ref, energy_ref, ws_ref, special_ref, ends_ref, mult_ref, support_ref, xb_ref, zb_ref) = take(9)
    if not last:
        xf_ref, zf_ref = take(2)
    if first:
        pieces = take(weights_of)
    else:
        sum_ref, mean_ref = take(2)
    misfit_ref = take(1)[0]
    if last:
        average_ref = take(1)[0]
    else:
        new_mean_ref, part_ref = take(2)
        if first:
            kept_ref = take(1)[0]
    (held_ref,) = take(1)
    n = ws_ref.shape[1]
    planes = ends_ref.shape[0]
    cells, volume_total = energy_ref[1, 0], energy_ref[2, 0]
    total = energy_ref[0:1, :]
    if not first:
        total = total + jnp.sum(parts_ref[...], axis=0, keepdims=True)
    total = jnp.sum(total)
    misfit = total / (volume_total * cells)
    misfit_ref[...] = jnp.full(misfit_ref.shape, misfit, F32)
    damping = REG_WEIGHT * volume_total * misfit + FLOOR_VALUE
    ws = ws_ref[0]
    ws_mirror = ws_ref[1]
    inverse = 1.0 / (ws + damping)
    inverse_mirror = 1.0 / (ws_mirror + damping)
    special = special_ref[...] > 0.5
    sums = []
    uppers = []
    for plane in range(planes):
        if first:
            per = planes // (2 * weights_of)
            color, inner = plane // (planes // 2), plane % (planes // 2)
            piece = pieces[inner // per]
            value = piece[0, color, inner % per]
            for source in range(1, piece.shape[0]):
                value = value + piece[source, color, inner % per]
            if not last:
                kept_ref[plane] = value
        else:
            value = sum_ref[plane]
        mirror = jnp.where(special, ends_ref[plane], value)
        sums.append((value, mirror))
        if first:
            upper = 0.5 * (value * inverse + mirror * inverse_mirror)
        else:
            pulled = damping * mean_ref[plane]
            upper = 0.5 * ((pulled + value) * inverse + (pulled + mirror) * inverse_mirror)
        uppers.append(upper)
    wide = times_right(jnp.concatenate(uppers, axis=0), xb_ref[...])
    high, low = split_value(wide)

    def z_step(table_ref, high, low):
        result = []
        for pair in range((planes + 1) // 2):
            members = [p for p in (2 * pair, 2 * pair + 1) if p < planes]
            field = times_left(
                table_ref[...],
                jnp.concatenate([stacked(high[p * n : (p + 1) * n], n) for p in members], axis=1),
                jnp.concatenate([stacked(low[p * n : (p + 1) * n], n) for p in members], axis=1),
            )
            result += [field[:, i * n : (i + 1) * n] for i in range(len(members))]
        return result

    fields = z_step(zb_ref, high, low)
    layer = support_ref.shape[2]
    averages = []
    for plane in range(planes):
        for slab in range(support_ref.shape[0]):
            piece = support_ref[slab, plane] * fields[plane][slab * layer : (slab + 1) * layer]
            if last:
                average_ref[slab, plane] = piece
            else:
                averages.append(piece)
    if last:
        return
    wide = times_right(jnp.concatenate(averages, axis=0), xf_ref[...])
    high, low = split_value(wide)
    means = z_step(zf_ref, high, low)
    ws_both = 0.5 * (ws + ws_mirror)
    acc = jnp.zeros((n, n), F32)
    for plane in range(planes):
        mean = means[plane]
        value, mirror = sums[plane]
        new_mean_ref[plane] = mean
        acc = acc + mean * (ws_both * mean - (value + mirror))
    acc = jnp.sum(acc * mult_ref[...], axis=0, keepdims=True)
    part_ref[...] = jnp.broadcast_to(acc, part_ref.shape)


def refine(first, last, parts, energy, ws, ends, support, pieces, peers):
    n = ws.shape[1]
    planes = ends.shape[0]
    slabs, _, layer, _ = support.shape
    kz, kx, edge = np_packed(n)
    special = (edge | (kz == n // 2)).astype(np.float32)
    lone = edge & (np.arange(n)[:, None] % (n // 2) == 0)
    mult = np.where(lone, 1.0, 2.0).astype(np.float32)
    args = [parts, energy, ws, special, ends, mult, support, np_right(np_x_backward(n)), np_left(np_z_backward(n))]
    if not last:
        args += [np_right(np_x_forward(n)), np_left(np_z_forward(n))]
    args += list(pieces)
    shape = lambda *dims: jax.ShapeDtypeStruct(dims, F32)
    outs = [shape(1, n)]
    if last:
        outs += [shape(slabs, planes, layer, n)]
    else:
        outs += [shape(planes, n, n), shape(peers, n)]
        if first:
            outs += [shape(planes, n, n)]
    return pl.pallas_call(
        functools.partial(refine_kernel, first, last, len(pieces), peers),
        out_shape=outs,
        in_specs=[pl.BlockSpec(memory_space=pltpu.VMEM)] + [pl.BlockSpec(memory_space=pltpu.SMEM) if False else pl.BlockSpec(memory_space=pltpu.VMEM)] * (len(args) - 1),
        out_specs=[pl.BlockSpec(memory_space=pltpu.VMEM)] * len(outs),
        scratch_shapes=[pltpu.VMEM((8, n), F32)],
        name="refine",
    )(*[jnp.asarray(arg) for arg in args])


def extras(volumes, info, start, order, n):
    half = n // 2
    layer = volumes.shape[1]
    kz, kx, _ = np_packed(n)
    theta = np_theta((n - kz) % n, (n - kx) % n, n)
    mirrored = wedge(info[:, 0], info[:, 1], jnp.asarray(theta))
    sign = lambda index: (1 - 2 * (index % 2)).astype(F32)
    x_sign = sign(jnp.arange(n, dtype=jnp.int32)[None, :] + info[:, 4:5])
    z_sign = sign(jnp.arange(layer, dtype=jnp.int32)[None, :] + start + info[:, 2:3])
    ends = jnp.stack([jnp.sum(volumes, axis=3), jnp.sum(volumes * x_sign[:, None, None, :], axis=3)], axis=1)
    middle = jnp.sum(volumes * z_sign[:, :, None, None], axis=1)
    z = jnp.arange(layer, dtype=jnp.int32)[None, None, :] + start + info[:, 2][:, None, None]
    k = np.arange(n)[:, None]
    row = np.where(k <= half, k, k - half)
    turns = (z * jnp.asarray(row, jnp.int32) + jnp.asarray(np.where(k <= half, 0, n // 4), jnp.int32)) % n
    z_table = jnp.cos(turns.astype(F32) * F32(2.0 * math.pi / n)) * F32(1.0 / n)
    columns = jnp.einsum("skz,sczy->syck", z_table, ends, precision=HIGHEST)
    columns = columns * jnp.stack([mirrored[:, :, 0], mirrored[:, :, half]], axis=1)[:, None]
    lane = np.arange(n)
    x = jnp.arange(n, dtype=jnp.int32)[None, :, None] + info[:, 4][:, None, None]
    turns = (x * jnp.asarray(lane % half, jnp.int32) + jnp.asarray(np.where(lane < half, 0, n // 4), jnp.int32)) % n
    x_table = jnp.cos(turns.astype(F32) * F32(2.0 * math.pi / n)) * F32(1.0 / n)
    across = jnp.einsum("syx,sxc->syc", middle, x_table, precision=HIGHEST) * mirrored[:, half, None, :]
    rows = jnp.concatenate([columns, across[:, :, None, :]], axis=2)
    place = (jnp.asarray(order, jnp.int32)[None, :] - info[:, 3:4]) % n
    chosen = (place[:, :, None] == jnp.arange(n, dtype=jnp.int32)).astype(F32)
    return jnp.einsum("spy,syck->pck", chosen, rows, precision=HIGHEST)


def end_planes(rows, n):
    half = n // 2
    lane = jnp.arange(n)[None, None, :]
    row = jnp.arange(n)[None, :, None]
    value = jnp.where((row == half), rows[:, 2, None, :], 0.0)
    value = jnp.where(lane == 0, rows[:, 0, :, None], value)
    return jnp.where(lane == half, rows[:, 1, :, None], value)


def squares(low, high, n):
    kz, kx, _ = np_packed(n)
    result = []
    for theta in (np_theta(kz, kx, n), np_theta((n - kz) % n, (n - kx) % n, n)):
        weight = wedge(low, high, jnp.asarray(theta))
        result.append(jnp.sum(weight * weight, axis=0))
    return jnp.stack(result)


def body(volumes, tilt_low, tilt_high, shifts, support):
    items, layer, n = volumes.shape[0], volumes.shape[1], volumes.shape[3]
    batches, slabs = lax.axis_size("batch"), lax.axis_size("slab")
    place, slab = lax.axis_index("batch"), lax.axis_index("slab")
    start = slab * layer
    subs = items * batches
    info = jnp.concatenate([tilt_low[:, None], tilt_high[:, None], shifts], axis=1)
    kz, kx, _ = np_packed(n)
    theta = jnp.asarray(np_theta(kz, kx, n))
    spread = batches == 8 and n % (8 * slabs * 2 * STREAMS) == 0
    swap = lambda value, bit: lax.ppermute(value, "batch", [(i, i ^ bit) for i in range(batches)])
    own_energy = jnp.sum(volumes * volumes)
    lanes = jnp.arange(n, dtype=jnp.int32)
    mine = lambda row: jnp.sum(
        jnp.where(lanes[None, :] == (place * items + jnp.arange(items, dtype=jnp.int32))[:, None], row.astype(F32)[:, None], 0.0), axis=0
    )

    if not spread:
        order = np.arange(n)
        right, left = shifted_tables(info[:, 2], info[:, 4], start, layer, n)
        weight = wedge(info[:, 0], info[:, 1], theta)
        source = (lanes[None, :] - info[:, 3:4]) % n
        (sums,) = gather_planes([volumes], source, right, left, weight, [n])
        sums = lax.psum_scatter(lax.psum(sums, "batch"), "slab", scatter_dimension=0, tiled=True)
        rows = extras(volumes, info, start, order, n)
        facts = jnp.stack([mine(info[:, 0]), mine(info[:, 1]), jnp.full((n,), own_energy)])
        rows, facts = lax.psum((rows, facts), ("batch", "slab"))
        planes = n // slabs
        rows = lax.dynamic_slice_in_dim(rows, slab * planes, planes, axis=0)
        pieces = [sums.reshape(1, 2, planes // 2, n, n)]
        support_planes = lax.all_to_all(support.transpose(1, 0, 2), "slab", split_axis=0, concat_axis=0, tiled=True)
        support_planes = support_planes.reshape(slabs, planes, layer, n)
        peers = 1
        share = lambda value: lax.psum(value, "slab")
    else:
        partner = swap(volumes, 1)
        partner_info = swap(info, 1)
        both = jnp.concatenate([info, partner_info], axis=0)
        right, left = shifted_tables(both[:, 2], both[:, 4], start, layer, n)
        weight = wedge(both[:, 0], both[:, 1], theta)
        core, at_x, at_y = place % 2, (place // 2) % 2, place // 4
        inner = n // (16 * slabs)
        per = inner // STREAMS

        def plane_of(core, color, at_y, at_x, at_z, at_j):
            return ((((core * 2 + color) * 2 + at_y) * 2 + at_x) * slabs + at_z) * inner + at_j

        at_z = np.arange(slabs)[:, None]
        sent, kept = [], []
        for stream in range(STREAMS):
            at_j = np.arange(per)[None, :] + stream * per
            for held, flip in ((sent, True), (kept, False)):
                targets = []
                near_x, near_y = (1 - at_x, 1 - at_y) if flip else (at_x, at_y)
                targets += [plane_of(core, 0, y, near_x, at_z, at_j).reshape(-1) for y in (1 - at_y, at_y)]
                targets += [plane_of(core, 1, near_y, x, at_z, at_j).reshape(-1) for x in (1 - at_x, at_x)]
                source = (jnp.concatenate(targets)[None, :] - both[:, 3:4]) % n
                count = 2 * slabs * per
                held.append(gather_planes([volumes, partner], source.astype(jnp.int32), right, left, weight, [count, count]))
        pieces = []
        for stream in range(STREAMS):
            halves = []
            for color, (near, far) in enumerate(((2, 4), (4, 2))):
                got = swap(sent[stream][color], near).reshape(2, slabs, per, n, n)
                own = kept[stream][color].reshape(2, slabs, per, n, n)
                second = swap(got[0] + own[0], far)
                halves.append(second + (got[1] + own[1]))
            pieces.append(lax.all_to_all(jnp.stack(halves, axis=1), "slab", split_axis=0, concat_axis=0, tiled=True))
        planes = 2 * inner
        index = np.arange(batches)
        order = plane_of(
            (index % 2)[:, None, None, None],
            np.arange(2)[None, None, :, None],
            (index // 4)[:, None, None, None],
            ((index // 2) % 2)[:, None, None, None],
            np.arange(slabs)[None, :, None, None],
            np.arange(inner)[None, None, None, :],
        ).reshape(-1)
        peers = batches * slabs
        rows = extras(volumes, info, start, order, n).reshape(peers, planes * 3, n)
        facts = jnp.stack([mine(info[:, 0]), mine(info[:, 1]), jnp.full((n,), own_energy)])
        packed = jnp.concatenate([rows, jnp.broadcast_to(facts[None], (peers, 3, n)), jnp.zeros((peers, -(planes * 3 + 3) % 8, n), F32)], axis=1)
        packed = lax.all_to_all(packed, ("batch", "slab"), split_axis=0, concat_axis=0, tiled=True)
        packed = jnp.sum(packed, axis=0)
        rows, facts = packed[: planes * 3].reshape(planes, 3, n), packed[planes * 3 : planes * 3 + 3]
        viewed = support.reshape(layer, 2, 2, 4, slabs, inner, n)
        viewed = lax.dynamic_slice(viewed, (0, core, 0, at_y * 2 + at_x, 0, 0, 0), (layer, 1, 2, 1, slabs, inner, n))
        viewed = viewed.reshape(layer, 2, slabs, inner, n).transpose(2, 1, 3, 0, 4).reshape(slabs, planes, layer, n)
        support_planes = lax.all_to_all(viewed, "slab", split_axis=0, concat_axis=0, tiled=True)
        share = lambda value: lax.all_to_all(value, ("batch", "slab"), split_axis=0, concat_axis=0, tiled=True)

    low = facts[0, :subs] / slabs
    high = facts[1, :subs] / slabs
    ws = squares(low, high, n)
    lane0 = (lanes == 0)[None, :]
    energy = jnp.concatenate(
        [jnp.where(lane0, facts[2:3], 0.0), jnp.full((1, n), float(n) ** 3, F32), jnp.full((1, n), float(subs), F32)], axis=0
    )
    ends = end_planes(rows, n)
    misfits = []
    parts = jnp.zeros((peers, n), F32)
    for turn in range(ITERS):
        first, last = turn == 0, turn + 1 == ITERS
        result = refine(first, last, parts, energy, ws, ends, support_planes, pieces, peers)
        misfits.append(result[0][0, 0])
        if last:
            average = result[1]
        else:
            if first:
                sums = result[3]
            pieces = (sums, result[1])
            parts = share(result[2])
    misfits = jnp.stack(misfits)

    average = lax.all_to_all(average, "slab", split_axis=0, concat_axis=0, tiled=True)
    if not spread:
        return average.transpose(2, 0, 1, 3).reshape(layer, n, n), misfits
    average = average.reshape(slabs, 2, inner, layer, n)
    blocks = []
    for color, (near, far) in enumerate(((2, 4), (4, 2))):
        own = average[:, color].reshape(slabs * inner, layer, n)
        got = swap(own, near)
        pair = jnp.stack([own, got])
        blocks.append(jnp.stack([pair, swap(pair, far)]))
    blocks = jnp.stack([blocks[0], blocks[1].transpose(1, 0, 2, 3, 4)])
    blocks = jnp.stack([blocks, swap(blocks, 1)])
    for axis, bit in ((0, core), (2, at_y), (3, at_x)):
        blocks = jnp.where(bit == 1, jnp.flip(blocks, axis), blocks)
    return blocks.transpose(5, 0, 1, 2, 3, 4, 6).reshape(layer, n, n), misfits


def solution(mesh):
    placed = (
        P("batch", "slab", None, None),
        P("batch"),
        P("batch"),
        P("batch", None),
        P("slab", None, None),
    )
    return jax.shard_map(
        body, mesh=mesh, in_specs=placed, out_specs=(P("slab", None, None), P()), check_vma=False
    )
```

time: 897 us -> 191 us (0.21)
  waiting for transfers between devices: 567 us -> 28.8 us
  matrix products: 121 us -> 1.82 us
  local copies, waits for them, and re-layouts: 62.4 us -> 7.86 us
  Pallas kernels: 0 us -> 39.7 us
  other arithmetic: 17 us -> 42.5 us
  between operations: 24.8 us -> 1.22 us
  starting transfers between devices: 51.8 us -> 32.7 us
  blocking collectives: 47.4 us -> 34.5 us
    all_to_all x11 -> x4, waiting for transfers between devices: 504 us -> 14.2 us  [the longest x2 14.2 us: body(): lax.all_to_all(jnp.stack(halves, axis=1), 'slab', split_axis=0, concat_ax...]
    dot_general x36 -> x3, matrix products: 121 us -> 1.82 us  [the longest x1 0.83 us: extras(): jnp.einsum('syx,sxc->syc', middle, x_table, precision=HIGHEST)]
    psum x1 -> x0, waiting for transfers between devices: 63.2 us -> none  [body(): lax.psum((part_real, part_imag, weight_square, energy), 'batch')]
    psum x4 -> x0, blocking collectives: 47.4 us -> none  [the longest x3 33.1 us: body(): total = lax.psum(local, 'slab')]
    pallas_call x0 -> x7, Pallas kernels: none -> 39.7 us  [the longest x4 28.8 us: gather_planes(): pl.pallas_call(functools.partial(gather_kernel, tuple((count // GROUP for...]
    all_to_all x0 -> x3, blocking collectives: none -> 34.5 us  [the longest x2 22.2 us: body(): lax.all_to_all(value, ('batch', 'slab'), split_axis=0, concat_axis=0, til...]
    all_to_all x11 -> x4, starting transfers between devices: 51.6 us -> 20.5 us  [the longest x2 8.28 us: body(): lax.all_to_all(jnp.stack(halves, axis=1), 'slab', split_axis=0, concat_ax...]
    all_to_all x11 -> x0, local copies, waits for them, and re-layouts: 26.1 us -> none  [the longest x3 9.55 us: body(): lax.all_to_all(imag_part, 'slab', split_axis=0, concat_axis=1, tiled=True)]
  transfers between devices with their start and end apart: 12 -> 19, of which waited for: 12 -> 8; matrix products, arithmetic and copies ran while one was open for 7% -> 23% of each run, Pallas kernels for 0% -> 15%
where the time goes in v1:
time: 191 us; the launch traced here: 189 us
  other arithmetic  42.5 us (22%)
  Pallas kernels  39.7 us (21%)
  blocking collectives  34.5 us (18%)
  starting transfers between devices  32.7 us (17%)
  waiting for transfers between devices  28.8 us (15%)
  local copies, waits for them, and re-layouts  7.86 us (4%)
    pallas_call x4, Pallas kernels, gather_planes(): pl.pallas_call(functools.partial(gather_kernel, tuple((count // GROUP for...  28.8 us
    all_to_all x2, blocking collectives, body(): lax.all_to_all(value, ('batch', 'slab'), split_axis=0, concat_axis=0, til...  22.2 us
    ppermute x15, waiting for transfers between devices, body(): lax.ppermute(value, 'batch', [(i, i ^ bit) for i in range(batches)])  14.6 us
    all_to_all x2, waiting for transfers between devices, body(): lax.all_to_all(jnp.stack(halves, axis=1), 'slab', split_axis=0, concat_ax...  14.2 us
    all_to_all x1, blocking collectives, body(): lax.all_to_all(average, 'slab', split_axis=0, concat_axis=0, tiled=True)  12.3 us
    ppermute x15, starting transfers between devices, body(): lax.ppermute(value, 'batch', [(i, i ^ bit) for i in range(batches)])  12.2 us
    pallas_call x3, Pallas kernels, refine(): pl.pallas_call(functools.partial(refine_kernel, first, last, len(pieces),...  10.9 us
    all_to_all x2, starting transfers between devices, body(): lax.all_to_all(jnp.stack(halves, axis=1), 'slab', split_axis=0, concat_ax...  8.28 us
  transfers between devices with their start and end apart: 19, of which 8 were waited for; matrix products, arithmetic and copies ran while one was open for 23% of the time, Pallas kernels for 15%

profile of v1, /device:TPU:0, one launch (start us, length us, event | category | flops | bytes accessed | tf_op | source)
XLA Modules:
  0.0 189.1 jit_solution(2227345789177444100)
XLA Ops:
  8.0 5.4 %fusion.141 = (f32[2,32,128]{2,1,0:T(8,128)S(1)}, f32[]{:T(128)}, f32[2,128,128]{2,1,0:T(8,128)S(1)}, f32[2,32,128]{2,1,0:T(8,128)S(1)}) fusion(f32[2,32,128,128]{3,2,1,0:T(8,128)} %rest_0_.7, f32[2,32]{1,0:T(2,128)S(1)} %get-tuple-element.75, f32[2,128]{1,0:T(2,128)S(1)} %get-tuple-element.97), kind=kLoop, calls=%fused_computation.281 | loop fusion | flops 7290879 | bytes 4392196 | tf_op jit(solution)/shard_map/reduce_sum | solution.py:368
  17.3 7.3 %all-to-all-start = ((f32[32,16,128]{2,1,0:T(8,128)}), f32[32,16,128]{2,1,0:T(8,128)S(1)}, u32[]{:S(2)}, u32[]{:S(2)}) async-start(f32[32,16,128]{2,1,0:T(8,128)} %maximum_maximum_fusion), calls=%async_computation | async-start | bytes 524288 | tf_op jit(solution)/shard_map/all_to_all | solution.py:488
  29.4 1.7 cosine_multiply_fusion
  32.5 3.2 %reduce-precision_convert_fusion = (bf16[4,128,384]{2,1,0:T(8,128)(2,1)S(1)}, bf16[4,128,384]{2,1,0:T(8,128)(2,1)S(1)}) fusion(f32[384]{0:T(512)S(1)} %copy-done.15, s32[384]{0:T(512)S(1)} %copy-done.14, s32[384]{0:T(512)S(1)} %copy-done.13, s32[4,128]{1,0:T(4,128)S(1)} %iota_add_fusion), kind=kLoop, calls=%fused_computation.17 | loop fusion | flops 3932160 | bytes 793088 | tf_op jit(solution)/shard_map/convert_element_type | solution.py:104
  38.6 4.9 %all-to-all-start.1 = ((f32[4,4,32,128]{3,2,1,0:T(8,128)}), f32[4,4,32,128]{3,2,1,0:T(8,128)S(1)}, u32[]{:S(2)}, u32[]{:S(2)}) async-start(f32[4,4,32,128]{3,2,1,0:T(8,128)} %bitcast.21), calls=%async_computation.1 | async-start | bytes 524288 | tf_op jit(solution)/shard_map/all_to_all | solution.py:494
  43.6 7.1 %gather_planes.6 = (f32[8,128,128]{2,1,0:T(8,128)}, f32[8,128,128]{2,1,0:T(8,128)}) custom-call(s32[4,16]{1,0:T(4,128)} %get-tuple-element.77.source_ref, bf16[4,384,384]{2,1,0:T(8,128)(2,1)} %pad_maximum_fusion.1.right_ref, bf16[4,128,288]{2,1,0:T(8,128)(2,1)} %pad_maximum_fusion.5.left_ref, f32[4,128,128]{2,1,0:T(8,128)} %fusion.46.weight_ref, ...), custom_call_target="tpu_custom_call" | custom-call | tf_op jit(solution)/shard_map/gather_planes/pallas_call | solution.py:218
  53.8 7.2 %gather_planes.4 = (f32[8,128,128]{2,1,0:T(8,128)}, f32[8,128,128]{2,1,0:T(8,128)}) custom-call(s32[4,16]{1,0:T(4,128)} %get-tuple-element.79.source_ref, bf16[4,384,384]{2,1,0:T(8,128)(2,1)} %pad_maximum_fusion.1.right_ref, bf16[4,128,288]{2,1,0:T(8,128)(2,1)} %pad_maximum_fusion.5.left_ref, f32[4,128,128]{2,1,0:T(8,128)} %fusion.46.weight_ref, ...), custom_call_target="tpu_custom_call" | custom-call | tf_op jit(solution)/shard_map/gather_planes/pallas_call | solution.py:218
  63.4 7.1 %gather_planes.7 = (f32[8,128,128]{2,1,0:T(8,128)}, f32[8,128,128]{2,1,0:T(8,128)}) custom-call(s32[4,16]{1,0:T(4,128)} %get-tuple-element.76.source_ref, bf16[4,384,384]{2,1,0:T(8,128)(2,1)} %pad_maximum_fusion.1.right_ref, bf16[4,128,288]{2,1,0:T(8,128)(2,1)} %pad_maximum_fusion.5.left_ref, f32[4,128,128]{2,1,0:T(8,128)} %fusion.46.weight_ref, ...), custom_call_target="tpu_custom_call" | custom-call | tf_op jit(solution)/shard_map/gather_planes/pallas_call | solution.py:218
  70.6 7.4 %gather_planes.5 = (f32[8,128,128]{2,1,0:T(8,128)}, f32[8,128,128]{2,1,0:T(8,128)}) custom-call(s32[4,16]{1,0:T(4,128)} %get-tuple-element.78.source_ref, bf16[4,384,384]{2,1,0:T(8,128)(2,1)} %pad_maximum_fusion.1.right_ref, bf16[4,128,288]{2,1,0:T(8,128)(2,1)} %pad_maximum_fusion.5.left_ref, f32[4,128,128]{2,1,0:T(8,128)} %fusion.46.weight_ref, ...), custom_call_target="tpu_custom_call" | custom-call | tf_op jit(solution)/shard_map/gather_planes/pallas_call | solution.py:218
  87.9 2.1 %collective-permute-done.9 = f32[4,1,128,128]{3,2,0,1:T(8,128)S(1)} collective-permute-done((f32[4,1,128,128]{3,2,0,1:T(8,128)S(1)}, f32[4,1,128,128]{3,2,0,1:T(8,128)S(1)}, u32[]{:S(2)}, u32[]{:S(2)}) %collective-permute-start.9) | collective-permute-done | bytes 262176 | tf_op jit(solution)/shard_map/ppermute | solution.py:416
  91.8 4.8 %all-to-all-start.3 = ((f32[4,2,1,128,128]{4,3,2,1,0:T(8,128)}), f32[4,2,1,128,128]{4,3,2,1,0:T(8,128)S(1)}, u32[]{:S(2)}, u32[]{:S(2)}) async-start(f32[4,2,1,128,128]{4,3,2,1,0:T(8,128)} %pad_maximum_fusion.4), calls=%async_computation.3 | async-start | bytes 1048576 | tf_op jit(solution)/shard_map/all_to_all | solution.py:473
  100.2 6.9 %all-to-all-done.3.refs_12_ = f32[4,2,1,128,128]{4,3,2,1,0:T(8,128)S(1)} async-done(((f32[4,2,1,128,128]{4,3,2,1,0:T(8,128)}), f32[4,2,1,128,128]{4,3,2,1,0:T(8,128)S(1)}, u32[]{:S(2)}, u32[]{:S(2)}) %all-to-all-start.3) | async-done | bytes 524320 | tf_op jit(solution)/shard_map/all_to_all | solution.py:473
  107.1 3.5 %all-to-all-start.2 = ((f32[4,2,1,128,128]{4,3,2,1,0:T(8,128)}), f32[4,2,1,128,128]{4,3,2,1,0:T(8,128)S(1)}, u32[]{:S(2)}, u32[]{:S(2)}) async-start(f32[4,2,1,128,128]{4,3,2,1,0:T(8,128)} %pad_maximum_fusion.3), calls=%async_computation.2 | async-start | bytes 1048576 | tf_op jit(solution)/shard_map/all_to_all | solution.py:473
  113.5 7.3 %all-to-all-done.2.refs_11_ = f32[4,2,1,128,128]{4,3,2,1,0:T(8,128)S(1)} async-done(((f32[4,2,1,128,128]{4,3,2,1,0:T(8,128)}), f32[4,2,1,128,128]{4,3,2,1,0:T(8,128)S(1)}, u32[]{:S(2)}, u32[]{:S(2)}) %all-to-all-start.2) | async-done | bytes 524320 | tf_op jit(solution)/shard_map/all_to_all | solution.py:473
  121.6 4.0 %refine.3 = (f32[1,128]{1,0:T(1,128)}, f32[4,128,128]{2,1,0:T(8,128)}, f32[32,128]{1,0:T(8,128)}, f32[4,128,128]{2,1,0:T(8,128)}) custom-call(f32[32,128]{1,0:T(8,128)} %broadcast_in_dim.77.refs_0_, f32[3,128]{1,0:T(4,128)} %maximum_maximum_fusion.2.refs_1_, f32[2,128,128]{2,1,0:T(8,128)} %pad_maximum_fusion.9.refs_2_, f32[128,128]{1,0:T(8,128)} %constant.253.clone.refs_3_, ...), custom_call_target="tpu_custom_call" | custom-call | tf_op jit(solution)/shard_map/refine/pallas_call | solution.py:349
  125.7 11.9 %all_to_all.47 = f32[32,1,128]{2,1,0:T(1,128)} all-to-all(f32[32,1,128]{2,1,0:T(1,128)} %bitcast.178), channel_id=1, replica_groups=mesh['batch'=8,'slab'=4] {'batch','slab'}, dimensions={0} | all-to-all | bytes 32768 | tf_op jit(solution)/shard_map/all_to_all | solution.py:495
  137.5 3.9 %refine.4 = (f32[1,128]{1,0:T(1,128)}, f32[4,128,128]{2,1,0:T(8,128)}, f32[32,128]{1,0:T(8,128)}) custom-call(f32[32,128]{1,0:T(8,128)} %bitcast.174, f32[3,128]{1,0:T(4,128)} %maximum_maximum_fusion.2.refs_1_, f32[2,128,128]{2,1,0:T(8,128)} %pad_maximum_fusion.9.refs_2_, f32[128,128]{1,0:T(8,128)} %constant.253.clone.refs_3_, ...), custom_call_target="tpu_custom_call" | custom-call | tf_op jit(solution)/shard_map/refine/pallas_call | solution.py:349
  141.4 10.3 %all_to_all.48 = f32[32,1,128]{2,1,0:T(1,128)} all-to-all(f32[32,1,128]{2,1,0:T(1,128)} %bitcast.179), channel_id=1, replica_groups=mesh['batch'=8,'slab'=4] {'batch','slab'}, dimensions={0} | all-to-all | bytes 32768 | tf_op jit(solution)/shard_map/all_to_all | solution.py:495
  151.7 3.0 %refine.5 = (f32[1,128]{1,0:T(1,128)}, f32[4,4,32,128]{3,2,1,0:T(8,128)}) custom-call(f32[32,128]{1,0:T(8,128)} %bitcast.173, f32[3,128]{1,0:T(4,128)} %maximum_maximum_fusion.2.refs_1_, f32[2,128,128]{2,1,0:T(8,128)} %pad_maximum_fusion.9.refs_2_, f32[128,128]{1,0:T(8,128)} %constant.253.clone.refs_3_, f32[4,128,128]{2,1,0:T(8,128)} %select_select_fusion.refs_4_, ...), custom_call_target="tpu_custom_call" | custom-call | tf_op jit(solution)/shard_map/refine/pallas_call | solution.py:349
  154.7 12.3 %all_to_all.49 = f32[4,4,32,128]{3,2,1,0:T(8,128)S(1)} all-to-all(f32[4,4,32,128]{3,2,1,0:T(8,128)} %get-tuple-element.32), channel_id=1, replica_groups=mesh['batch'=8,'slab'=4] {'slab'}, dimensions={0} | all-to-all | bytes 524288 | tf_op jit(solution)/shard_map/all_to_all | solution.py:520
  168.7 3.6 %collective-permute-done.10 = f32[8,32,128]{2,0,1:T(8,128)S(1)} collective-permute-done((f32[8,32,128]{2,0,1:T(8,128)S(1)}, f32[8,32,128]{2,0,1:T(8,128)S(1)}, u32[]{:S(2)}, u32[]{:S(2)}) %collective-permute-start.10) | collective-permute-done | bytes 131104 | tf_op jit(solution)/shard_map/ppermute | solution.py:416
  175.9 2.9 %collective-permute-done.11 = f32[2,8,32,128]{3,1,0,2:T(8,128)S(1)} collective-permute-done((f32[2,8,32,128]{3,1,0,2:T(8,128)S(1)}, f32[2,8,32,128]{3,1,0,2:T(8,128)S(1)}, u32[]{:S(2)}, u32[]{:S(2)}) %collective-permute-start.11) | collective-permute-done | bytes 262176 | tf_op jit(solution)/shard_map/ppermute | solution.py:416
  178.8 2.1 %collective-permute-done.13 = f32[2,8,32,128]{3,1,0,2:T(8,128)S(1)} collective-permute-done((f32[2,8,32,128]{3,1,0,2:T(8,128)S(1)}, f32[2,8,32,128]{3,1,0,2:T(8,128)S(1)}, u32[]{:S(2)}, u32[]{:S(2)}) %collective-permute-start.13) | collective-permute-done | bytes 262176 | tf_op jit(solution)/shard_map/ppermute | solution.py:416
  182.9 2.4 %collective-permute-done.14 = f32[2,2,2,8,32,128]{5,3,2,1,0,4:T(8,128)} collective-permute-done((f32[2,2,2,8,32,128]{5,3,2,1,0,4:T(8,128)}, f32[2,2,2,8,32,128]{5,3,2,1,0,4:T(8,128)}, u32[]{:S(2)}, u32[]{:S(2)}) %collective-permute-start.14) | collective-permute-done | bytes 1048608 | tf_op jit(solution)/shard_map/ppermute | solution.py:416
  (162 shorter events, 55.6 us)
Async XLA Ops:
  0.6 24.1 %copy-start = (f32[32,128,128]{2,1,0:T(8,128)S(1)}, f32[32,128,128]{2,1,0:T(8,128)}, u32[]{:S(2)}) copy-start(f32[32,128,128]{2,1,0:T(8,128)} %param.46) | copy-start | bytes 6291460
  3.0 24.5 %collective-permute-start = (s32[2,5]{1,0:T(2,128)S(1)}, s32[2,5]{1,0:T(2,128)S(1)}, u32[]{:S(2)}, u32[]{:S(2)}) collective-permute-start(s32[2,5]{1,0:T(2,128)S(1)} %pad_add_fusion.1), channel_id=1, source_target_pairs={{0,4},{4,0},{8,12},{12,8},{16,20},{20,16},{24,28},{28,24},{1,5},{5... | collective-permute-start | bytes 128 | tf_op jit(solution)/shard_map/ppermute | solution.py:416
  3.5 40.0 %collective-permute-start.1 = (f32[2,32,128,128]{3,2,1,0:T(8,128)}, f32[2,32,128,128]{3,2,1,0:T(8,128)}, u32[]{:S(2)}, u32[]{:S(2)}) collective-permute-start(f32[2,32,128,128]{3,2,1,0:T(8,128)} %rest_0_.7), channel_id=1, source_target_pairs={{0,4},{4,0},{8,12},{12,8},{16,20},{20,16},{24,28},{28,24},{1,5},{5... | collective-permute-start | bytes 12582920 | tf_op jit(solution)/shard_map/ppermute | solution.py:416
  14.3 13.1 %copy-start.20 = (s32[4,1]{0,1:T(1,128)S(1)}, s32[4,1]{0,1:T(1,128)}, u32[]{:S(2)}) copy-start(s32[4,1]{0,1:T(1,128)} %constant.246.clone) | copy-start | bytes 52
  17.3 21.3 %all-to-all-start = ((f32[32,16,128]{2,1,0:T(8,128)}), f32[32,16,128]{2,1,0:T(8,128)S(1)}, u32[]{:S(2)}, u32[]{:S(2)}) async-start(f32[32,16,128]{2,1,0:T(8,128)} %maximum_maximum_fusion), calls=%async_computation | async-start | bytes 524288 | tf_op jit(solution)/shard_map/all_to_all | solution.py:488
  38.6 53.2 %all-to-all-start.1 = ((f32[4,4,32,128]{3,2,1,0:T(8,128)}), f32[4,4,32,128]{3,2,1,0:T(8,128)S(1)}, u32[]{:S(2)}, u32[]{:S(2)}) async-start(f32[4,4,32,128]{3,2,1,0:T(8,128)} %bitcast.21), calls=%async_computation.1 | async-start | bytes 524288 | tf_op jit(solution)/shard_map/all_to_all | solution.py:494
  50.7 27.3 %collective-permute-start.6 = (f32[8,128,128]{2,1,0:T(8,128)}, f32[8,128,128]{2,1,0:T(8,128)}, u32[]{:S(2)}, u32[]{:S(2)}) collective-permute-start(f32[8,128,128]{2,1,0:T(8,128)} %get-tuple-element.23), channel_id=1, source_target_pairs={{0,8},{4,12},{8,0},{12,4},{16,24},{20,28},{24,16},{28,20},{1,9},{5... | collective-permute-start | bytes 1572872 | tf_op jit(solution)/shard_map/ppermute | solution.py:416
  52.3 28.4 %collective-permute-start.8 = (f32[8,128,128]{2,1,0:T(8,128)}, f32[8,128,128]{2,1,0:T(8,128)}, u32[]{:S(2)}, u32[]{:S(2)}) collective-permute-start(f32[8,128,128]{2,1,0:T(8,128)} %get-tuple-element.25), channel_id=1, source_target_pairs={{0,16},{4,20},{8,24},{12,28},{16,0},{20,4},{24,8},{28,12},{1,17},{... | collective-permute-start | bytes 1572872 | tf_op jit(solution)/shard_map/ppermute | solution.py:416
  61.0 22.3 %collective-permute-start.2 = (f32[8,128,128]{2,1,0:T(8,128)}, f32[8,128,128]{2,1,0:T(8,128)S(1)}, u32[]{:S(2)}, u32[]{:S(2)}) collective-permute-start(f32[8,128,128]{2,1,0:T(8,128)} %get-tuple-element.19), channel_id=1, source_target_pairs={{0,8},{4,12},{8,0},{12,4},{16,24},{20,28},{24,16},{28,20},{1,9},{5... | collective-permute-start | bytes 1572872 | tf_op jit(solution)/shard_map/ppermute | solution.py:416
  62.8 22.7 %collective-permute-start.4 = (f32[8,128,128]{2,1,0:T(8,128)}, f32[8,128,128]{2,1,0:T(8,128)S(1)}, u32[]{:S(2)}, u32[]{:S(2)}) collective-permute-start(f32[8,128,128]{2,1,0:T(8,128)} %get-tuple-element.21), channel_id=1, source_target_pairs={{0,16},{4,20},{8,24},{12,28},{16,0},{20,4},{24,8},{28,12},{1,17},{... | collective-permute-start | bytes 1572872 | tf_op jit(solution)/shard_map/ppermute | solution.py:416
  79.1 7.7 %collective-permute-start.7 = (f32[4,1,128,128]{3,2,0,1:T(8,128)S(1)}, f32[4,1,128,128]{3,2,0,1:T(8,128)S(1)}, u32[]{:S(2)}, u32[]{:S(2)}) collective-permute-start(f32[4,1,128,128]{3,2,0,1:T(8,128)S(1)} %fusion.33), channel_id=1, source_target_pairs={{0,16},{4,20},{8,24},{12,28},{16,0},{20,4},{24,8},{28,12},{1,17},{... | collective-permute-start | bytes 786440 | tf_op jit(solution)/shard_map/ppermute | solution.py:416
  81.8 8.2 %collective-permute-start.9 = (f32[4,1,128,128]{3,2,0,1:T(8,128)S(1)}, f32[4,1,128,128]{3,2,0,1:T(8,128)S(1)}, u32[]{:S(2)}, u32[]{:S(2)}) collective-permute-start(f32[4,1,128,128]{3,2,0,1:T(8,128)S(1)} %fusion.29), channel_id=1, source_target_pairs={{0,8},{4,12},{8,0},{12,4},{16,24},{20,28},{24,16},{28,20},{1,9},{5... | collective-permute-start | bytes 786440 | tf_op jit(solution)/shard_map/ppermute | solution.py:416
  85.0 12.2 %collective-permute-start.3 = (f32[4,1,128,128]{3,2,0,1:T(8,128)}, f32[4,1,128,128]{3,2,0,1:T(8,128)}, u32[]{:S(2)}, u32[]{:S(2)}) collective-permute-start(f32[4,1,128,128]{3,2,0,1:T(8,128)} %fusion.41), channel_id=1, source_target_pairs={{0,16},{4,20},{8,24},{12,28},{16,0},{20,4},{24,8},{28,12},{1,17},{... | collective-permute-start | bytes 786440 | tf_op jit(solution)/shard_map/ppermute | solution.py:416
  86.3 11.9 %collective-permute-start.5 = (f32[4,1,128,128]{3,2,0,1:T(8,128)}, f32[4,1,128,128]{3,2,0,1:T(8,128)}, u32[]{:S(2)}, u32[]{:S(2)}) collective-permute-start(f32[4,1,128,128]{3,2,0,1:T(8,128)} %fusion.37), channel_id=1, source_target_pairs={{0,8},{4,12},{8,0},{12,4},{16,24},{20,28},{24,16},{28,20},{1,9},{5... | collective-permute-start | bytes 786440 | tf_op jit(solution)/shard_map/ppermute | solution.py:416
  91.8 15.3 %all-to-all-start.3 = ((f32[4,2,1,128,128]{4,3,2,1,0:T(8,128)}), f32[4,2,1,128,128]{4,3,2,1,0:T(8,128)S(1)}, u32[]{:S(2)}, u32[]{:S(2)}) async-start(f32[4,2,1,128,128]{4,3,2,1,0:T(8,128)} %pad_maximum_fusion.4), calls=%async_computation.3 | async-start | bytes 1048576 | tf_op jit(solution)/shard_map/all_to_all | solution.py:473
  97.1 15.4 %copy-start.18 = (pred[128]{0:T(512)(128)(4,1)S(1)}, pred[128]{0:T(512)(128)(4,1)}, u32[]{:S(2)}) copy-start(pred[128]{0:T(512)(128)(4,1)} %get-tuple-element.100) | copy-start | bytes 388
  97.1 15.4 %copy-start.19 = (pred[128]{0:T(512)(128)(4,1)S(1)}, pred[128]{0:T(512)(128)(4,1)}, u32[]{:S(2)}) copy-start(pred[128]{0:T(512)(128)(4,1)} %get-tuple-element.99) | copy-start | bytes 388
  107.1 14.4 %copy-start.2 = (f32[4,2,1,128,128]{4,3,2,1,0:T(8,128)}, f32[4,2,1,128,128]{4,3,2,1,0:T(8,128)S(1)}, u32[]{:S(2)}) copy-start(f32[4,2,1,128,128]{4,3,2,1,0:T(8,128)S(1)} %all-to-all-done.3.refs_12_) | copy-start | bytes 1572868
  107.1 13.7 %all-to-all-start.2 = ((f32[4,2,1,128,128]{4,3,2,1,0:T(8,128)}), f32[4,2,1,128,128]{4,3,2,1,0:T(8,128)S(1)}, u32[]{:S(2)}, u32[]{:S(2)}) async-start(f32[4,2,1,128,128]{4,3,2,1,0:T(8,128)} %pad_maximum_fusion.3), calls=%async_computation.2 | async-start | bytes 1048576 | tf_op jit(solution)/shard_map/all_to_all | solution.py:473
  167.1 5.1 %collective-permute-start.10 = (f32[8,32,128]{2,0,1:T(8,128)S(1)}, f32[8,32,128]{2,0,1:T(8,128)S(1)}, u32[]{:S(2)}, u32[]{:S(2)}) collective-permute-start(f32[8,32,128]{2,0,1:T(8,128)S(1)} %copy.144), channel_id=1, source_target_pairs={{0,8},{4,12},{8,0},{12,4},{16,24},{20,28},{24,16},{28,20},{1,9},{5... | collective-permute-start | bytes 393224 | tf_op jit(solution)/shard_map/ppermute | solution.py:416
  168.0 6.4 %collective-permute-start.12 = (f32[8,32,128]{2,0,1:T(8,128)S(1)}, f32[8,32,128]{2,0,1:T(8,128)S(1)}, u32[]{:S(2)}, u32[]{:S(2)}) collective-permute-start(f32[8,32,128]{2,0,1:T(8,128)S(1)} %copy.147), channel_id=1, source_target_pairs={{0,16},{4,20},{8,24},{12,28},{16,0},{20,4},{24,8},{28,12},{1,17},{... | collective-permute-start | bytes 393224 | tf_op jit(solution)/shard_map/ppermute | solution.py:416
  172.3 6.4 %collective-permute-start.11 = (f32[2,8,32,128]{3,1,0,2:T(8,128)S(1)}, f32[2,8,32,128]{3,1,0,2:T(8,128)S(1)}, u32[]{:S(2)}, u32[]{:S(2)}) collective-permute-start(f32[2,8,32,128]{3,1,0,2:T(8,128)S(1)} %get-tuple-element.59), channel_id=1, source_target_pairs={{0,16},{4,20},{8,24},{12,28},{16,0},{20,4},{24,8},{28,12},{1,17},{... | collective-permute-start | bytes 786440 | tf_op jit(solution)/shard_map/ppermute | solution.py:416
  174.5 6.4 %collective-permute-start.13 = (f32[2,8,32,128]{3,1,0,2:T(8,128)S(1)}, f32[2,8,32,128]{3,1,0,2:T(8,128)S(1)}, u32[]{:S(2)}, u32[]{:S(2)}) collective-permute-start(f32[2,8,32,128]{3,1,0,2:T(8,128)S(1)} %get-tuple-element.63), channel_id=1, source_target_pairs={{0,8},{4,12},{8,0},{12,4},{16,24},{20,28},{24,16},{28,20},{1,9},{5... | collective-permute-start | bytes 786440 | tf_op jit(solution)/shard_map/ppermute | solution.py:416
  182.2 3.0 %collective-permute-start.14 = (f32[2,2,2,8,32,128]{5,3,2,1,0,4:T(8,128)}, f32[2,2,2,8,32,128]{5,3,2,1,0,4:T(8,128)}, u32[]{:S(2)}, u32[]{:S(2)}) collective-permute-start(f32[2,2,2,8,32,128]{5,3,2,1,0,4:T(8,128)} %get-tuple-element.55), channel_id=1, source_target_pairs={{0,4},{4,0},{8,12},{12,8},{16,20},{20,16},{24,28},{28,24},{1,5},{5... | collective-permute-start | bytes 3145736 | tf_op jit(solution)/shard_map/ppermute | solution.py:416
  (21 other events, 125.8 us)
